TPU v7x, 32 devices: a whole 2x2x4 slice. The times are simulated.
32 devices in a mesh: tm: 4 (over x, core), anta: 4 (over z), antb: 2 (over y).
Axes of the slice: x: 2, y: 2, z: 4, core: 2. Of those that a mesh axis runs over, the one named last changes fastest.
Arguments:
- samples: bfloat16 [2, 512, 6144], P('antb', 'anta', 'tm'), may hold values from -6 to 6
Outputs:
- correlation: float32 [256, 2, 512, 2, 512], P('tm', None, 'anta', 'antb')
All inputs are finite; a program needn't handle non-finite values.
Results may differ from a plain program's by a relative error of at most 0.0003.
Values may be sent and summed in bfloat16 or wider, within the bound.
A program may use at most 128 MiB of HBM per device.

v0:
```python
import math
import jax
import jax.numpy as jnp
from jax import lax
from jax.sharding import PartitionSpec as P

ANTENNA_COUNT = 512
POLARISATION_NUM = 2
LAG_TOTAL = 256


def lag_terms(row_padded, columns, lag_start, lag_count, window_len):
    group_len = math.gcd(lag_count, 8)
    flat_cols = columns.reshape(columns.shape[1], columns.shape[2])

    def one_group(group_index):
        first_lag = lag_start + group_index * group_len
        pieces = [
            lax.dynamic_slice_in_dim(row_padded, LAG_TOTAL - first_lag - step_index, window_len, 1)
            for step_index in range(group_len)
        ]
        stacked = jnp.stack(pieces, 0)
        return jnp.einsum("kit,jt->kij", stacked, flat_cols, preferred_element_type=jnp.float32)

    grouped = lax.map(one_group, jnp.arange(lag_count // group_len, dtype=jnp.int32))
    return grouped.reshape(lag_count, row_padded.shape[0], flat_cols.shape[0])


def collect_rows(own_window):
    return lax.all_gather(own_window, "antb", axis=0, tiled=True)


def per_device(samples):
    antenna_total = samples.shape[1]
    block_len = samples.shape[2]
    tm_size = lax.axis_size("tm")
    lag_portion = LAG_TOTAL // tm_size
    full_length = block_len * tm_size
    factor = 1.0 / math.sqrt(full_length)
    lag_start = lax.axis_index("tm") * lag_portion
    col_tiles = lax.all_gather(samples, "anta", axis=1, tiled=True)
    columns = lax.all_gather(col_tiles, "tm", axis=2, tiled=True)
    own_rows = lax.dynamic_slice_in_dim(
        columns, lax.axis_index("anta") * antenna_total, antenna_total, 1
    )
    row_samples = collect_rows(own_rows)
    row_padded = jnp.pad(
        row_samples.reshape(POLARISATION_NUM * antenna_total, full_length), ((0, 0), (LAG_TOTAL, 0))
    )
    lag_group_block = lag_terms(row_padded, columns, lag_start, lag_portion, full_length)
    accumulated_sum = lag_group_block.reshape(
        lag_portion, POLARISATION_NUM, antenna_total, 1, ANTENNA_COUNT
    )
    return accumulated_sum * factor


def solution(mesh):
    return jax.shard_map(
        per_device,
        mesh=mesh,
        in_specs=(P("antb", "anta", "tm"),),
        out_specs=P("tm", None, "anta", "antb", None),
        check_vma=False,
    )
```

profile of v0, /device:TPU:0, one launch (start us, length us, event | category | flops | bytes accessed | tf_op | source)
XLA Modules:
  0.0 584.9 jit_solution(11511170079034413192)
XLA Ops:
  7.3 41.4 %all-gather.4.cloned.1.call-done = bf16[1,512,1536]{2,1,0:T(8,128)(2,1)} async-done(((bf16[1,128,1536]{2,1,0:T(8,128)(2,1)}), bf16[1,512,1536]{2,1,0:T(8,128)(2,1)}) %all-gather.4.cloned.1.call-update) | async-done | bytes 1572880 | tf_op jit(solution)/shard_map/all_gather | solution.py:41
  48.8 46.7 %all-gather.6.cloned.1.call-done = bf16[1,512,6144]{2,1,0:T(8,128)(2,1)} async-done(((bf16[1,512,1536]{2,1,0:T(8,128)(2,1)}), bf16[1,512,6144]{2,1,0:T(8,128)(2,1)}) %all-gather.6.cloned.1.call-update) | async-done | bytes 6291472 | tf_op jit(solution)/shard_map/all_gather | solution.py:42
  98.2 45.1 %all-gather.8.cloned.1.call-done = bf16[2,128,6144]{2,1,0:T(8,128)(2,1)} async-done(((bf16[1,128,6144]{2,1,0:T(8,128)(2,1)}), bf16[2,128,6144]{2,1,0:T(8,128)(2,1)}) %all-gather.8.cloned.1.call-update) | async-done | bytes 3145744 | tf_op jit(solution)/shard_map/all_gather | solution.py:30
  145.4 360.6 %while.14 = (s32[]{:T(128)}, f32[8,8,256,512]{3,2,1,0:T(8,128)}, s32[8]{0:T(128)S(1)}, s32[]{:T(128)}, bf16[256,6400]{1,0:T(8,128)(2,1)S(1)}, /*index=5*/bf16[51...) while((s32[]{:T(128)}, f32[8,8,256,512]{3,2,1,0:T(8,128)}, ...), condition=%wide.region_1.2_spmd, body=%wide.region_0.1_spmd.sunk | while | flops 12884901888 | bytes 85984392 | solution.py:25
  149.5 2.9 bitcast_dynamic-update-slice_fusion.19
  152.4 2.9 bitcast_dynamic-update-slice_fusion.20
  169.4 21.0 %bitcast_dynamic-update-slice_fusion.26 = f32[8,8,256,512]{3,2,1,0:T(8,128)} fusion(f32[8,8,256,512]{3,2,1,0:T(8,128)} %get-tuple-element.216, s32[]{:T(128)} %get-tuple-element.215, bf16[8,256,6144]{2,1,0:T(8,128)(2,1)} %bitcast_dynamic-update-slice_fusion.25, bf16[512,6144]{1,0:T(8,128)(2,1)} %get-tuple-element.245), kind=kOutput, calls=%fused_computation.2.clone.1 | convolution fusion | flops 12884901888 | bytes 35652096 | tf_op jit(solution)/shard_map/while/body/eval_jaxpr/kit,jt->kij/dot_general | solution.py:23
  194.6 2.9 bitcast_dynamic-update-slice_fusion.19
  197.5 2.9 bitcast_dynamic-update-slice_fusion.20
  214.5 21.1 %bitcast_dynamic-update-slice_fusion.26 = f32[8,8,256,512]{3,2,1,0:T(8,128)} fusion(f32[8,8,256,512]{3,2,1,0:T(8,128)} %get-tuple-element.216, s32[]{:T(128)} %get-tuple-element.215, bf16[8,256,6144]{2,1,0:T(8,128)(2,1)} %bitcast_dynamic-update-slice_fusion.25, bf16[512,6144]{1,0:T(8,128)(2,1)} %get-tuple-element.245), kind=kOutput, calls=%fused_computation.2.clone.1 | convolution fusion | flops 12884901888 | bytes 35652096 | tf_op jit(solution)/shard_map/while/body/eval_jaxpr/kit,jt->kij/dot_general | solution.py:23
  236.8 2.8 bitcast_dynamic-update-slice_fusion.18
  239.7 2.9 bitcast_dynamic-update-slice_fusion.19
  242.6 2.9 bitcast_dynamic-update-slice_fusion.20
  259.6 21.1 %bitcast_dynamic-update-slice_fusion.26 = f32[8,8,256,512]{3,2,1,0:T(8,128)} fusion(f32[8,8,256,512]{3,2,1,0:T(8,128)} %get-tuple-element.216, s32[]{:T(128)} %get-tuple-element.215, bf16[8,256,6144]{2,1,0:T(8,128)(2,1)} %bitcast_dynamic-update-slice_fusion.25, bf16[512,6144]{1,0:T(8,128)(2,1)} %get-tuple-element.245), kind=kOutput, calls=%fused_computation.2.clone.1 | convolution fusion | flops 12884901888 | bytes 35652096 | tf_op jit(solution)/shard_map/while/body/eval_jaxpr/kit,jt->kij/dot_general | solution.py:23
  281.9 2.8 bitcast_dynamic-update-slice_fusion.18
  284.8 2.9 bitcast_dynamic-update-slice_fusion.19
  287.6 2.9 bitcast_dynamic-update-slice_fusion.20
  304.7 21.1 %bitcast_dynamic-update-slice_fusion.26 = f32[8,8,256,512]{3,2,1,0:T(8,128)} fusion(f32[8,8,256,512]{3,2,1,0:T(8,128)} %get-tuple-element.216, s32[]{:T(128)} %get-tuple-element.215, bf16[8,256,6144]{2,1,0:T(8,128)(2,1)} %bitcast_dynamic-update-slice_fusion.25, bf16[512,6144]{1,0:T(8,128)(2,1)} %get-tuple-element.245), kind=kOutput, calls=%fused_computation.2.clone.1 | convolution fusion | flops 12884901888 | bytes 35652096 | tf_op jit(solution)/shard_map/while/body/eval_jaxpr/kit,jt->kij/dot_general | solution.py:23
  329.8 2.9 bitcast_dynamic-update-slice_fusion.19
  332.7 2.9 bitcast_dynamic-update-slice_fusion.20
  349.7 21.1 %bitcast_dynamic-update-slice_fusion.26 = f32[8,8,256,512]{3,2,1,0:T(8,128)} fusion(f32[8,8,256,512]{3,2,1,0:T(8,128)} %get-tuple-element.216, s32[]{:T(128)} %get-tuple-element.215, bf16[8,256,6144]{2,1,0:T(8,128)(2,1)} %bitcast_dynamic-update-slice_fusion.25, bf16[512,6144]{1,0:T(8,128)(2,1)} %get-tuple-element.245), kind=kOutput, calls=%fused_computation.2.clone.1 | convolution fusion | flops 12884901888 | bytes 35652096 | tf_op jit(solution)/shard_map/while/body/eval_jaxpr/kit,jt->kij/dot_general | solution.py:23
  374.9 2.9 bitcast_dynamic-update-slice_fusion.19
  377.8 2.9 bitcast_dynamic-update-slice_fusion.20
  394.8 21.1 %bitcast_dynamic-update-slice_fusion.26 = f32[8,8,256,512]{3,2,1,0:T(8,128)} fusion(f32[8,8,256,512]{3,2,1,0:T(8,128)} %get-tuple-element.216, s32[]{:T(128)} %get-tuple-element.215, bf16[8,256,6144]{2,1,0:T(8,128)(2,1)} %bitcast_dynamic-update-slice_fusion.25, bf16[512,6144]{1,0:T(8,128)(2,1)} %get-tuple-element.245), kind=kOutput, calls=%fused_computation.2.clone.1 | convolution fusion | flops 12884901888 | bytes 35652096 | tf_op jit(solution)/shard_map/while/body/eval_jaxpr/kit,jt->kij/dot_general | solution.py:23
  420.0 2.9 bitcast_dynamic-update-slice_fusion.19
  422.9 2.9 bitcast_dynamic-update-slice_fusion.20
  439.9 21.1 %bitcast_dynamic-update-slice_fusion.26 = f32[8,8,256,512]{3,2,1,0:T(8,128)} fusion(f32[8,8,256,512]{3,2,1,0:T(8,128)} %get-tuple-element.216, s32[]{:T(128)} %get-tuple-element.215, bf16[8,256,6144]{2,1,0:T(8,128)(2,1)} %bitcast_dynamic-update-slice_fusion.25, bf16[512,6144]{1,0:T(8,128)(2,1)} %get-tuple-element.245), kind=kOutput, calls=%fused_computation.2.clone.1 | convolution fusion | flops 12884901888 | bytes 35652096 | tf_op jit(solution)/shard_map/while/body/eval_jaxpr/kit,jt->kij/dot_general | solution.py:23
  465.1 2.9 bitcast_dynamic-update-slice_fusion.19
  467.9 2.9 bitcast_dynamic-update-slice_fusion.20
  485.0 21.1 %bitcast_dynamic-update-slice_fusion.26 = f32[8,8,256,512]{3,2,1,0:T(8,128)} fusion(f32[8,8,256,512]{3,2,1,0:T(8,128)} %get-tuple-element.216, s32[]{:T(128)} %get-tuple-element.215, bf16[8,256,6144]{2,1,0:T(8,128)(2,1)} %bitcast_dynamic-update-slice_fusion.25, bf16[512,6144]{1,0:T(8,128)(2,1)} %get-tuple-element.245), kind=kOutput, calls=%fused_computation.2.clone.1 | convolution fusion | flops 12884901888 | bytes 35652096 | tf_op jit(solution)/shard_map/while/body/eval_jaxpr/kit,jt->kij/dot_general | solution.py:23
  506.0 23.9 %broadcast_multiply_fusion = f32[8,8,256,512]{3,2,1,0:T(8,128)} fusion(f32[8,8,256,512]{3,2,1,0:T(8,128)} %get-tuple-element.140), kind=kLoop, calls=%fused_computation.11 | loop fusion | flops 8388608 | bytes 67108864 | tf_op jit(solution)/shard_map/mul | solution.py:54
  530.0 48.4 %mul.39 = f32[64,2,128,1,512]{4,3,2,1,0:T(1,128)} reshape(f32[8,8,256,512]{3,2,1,0:T(8,128)} %broadcast_multiply_fusion) | data formatting | bytes 67108864 | tf_op jit(solution)/shard_map/mul | solution.py:54
  (64 shorter events, 141.0 us)
Async XLA Ops:
  6.5 42.1 %all-gather.4.cloned.1.call-start = ((), (), s32[]{:S(2)}) async-start(), calls=%async_computation | async-start | bytes 1966080 | tf_op jit(solution)/shard_map/all_gather | solution.py:41
  7.3 88.2 %all-gather.6.cloned.1.call-start = ((), (), s32[]{:S(2)}) async-start(), calls=%async_computation.1 | async-start | bytes 7864320 | tf_op jit(solution)/shard_map/all_gather | solution.py:42
  48.7 94.6 %all-gather.8.cloned.1.call-start = ((), (), s32[]{:S(2)}) async-start(), calls=%async_computation.2 | async-start | bytes 4718592 | tf_op jit(solution)/shard_map/all_gather | solution.py:30
Sparse Core Ops, SparseCore 0:
  8.9 39.7 all-gather.3
  50.2 45.2 all-gather.5
  98.3 44.9 all-gather.7
where the time goes:
time: 586 us; the launch traced here: 585 us
  local copies, waits for them, and re-layouts  240 us (41%)
  matrix products  168 us (29%)
  waiting for transfers between devices  134 us (23%)
  other arithmetic  23.9 us (4%)
  between operations  13.1 us (2%)
    dot_general x8, matrix products, one_group(): jnp.einsum('kit,jt->kij', stacked, flat_cols, preferred_element_type=jnp....  168 us
    while x56, local copies, waits for them, and re-layouts  159 us
    mul x1, local copies, waits for them, and re-layouts, per_device(): return accumulated_sum * factor  48.4 us
    all_gather x1, waiting for transfers between devices, per_device(): columns = lax.all_gather(col_tiles, 'tm', axis=2, tiled=True)  46.7 us
    all_gather x1, waiting for transfers between devices, collect_rows(): return lax.all_gather(own_window, 'antb', axis=0, tiled=True)  45.1 us
    all_gather x1, waiting for transfers between devices, per_device(): col_tiles = lax.all_gather(samples, 'anta', axis=1, tiled=True)  41.4 us
    mul x1, other arithmetic, per_device(): return accumulated_sum * factor  23.9 us
    another operation x8, local copies, waits for them, and re-layouts, one_group(): stacked = jnp.stack(pieces, 0)  22.7 us
  transfers between devices with their start and end apart: 3, of which 3 were waited for; matrix products, arithmetic and copies ran while one was open for 0% of the time, Pallas kernels for 0%

commit v1 on v0

--- a/solution.py
+++ b/solution.py
@@ -38,7 +38,8 @@
     full_length = block_len * tm_size
     factor = 1.0 / math.sqrt(full_length)
     lag_start = lax.axis_index("tm") * lag_portion
-    col_tiles = lax.all_gather(samples, "anta", axis=1, tiled=True)
+    r1 = lax.all_gather(samples, "anta")
+    col_tiles = jnp.concatenate(r1, 1)
     columns = lax.all_gather(col_tiles, "tm", axis=2, tiled=True)
     own_rows = lax.dynamic_slice_in_dim(
         columns, lax.axis_index("anta") * antenna_total, antenna_total, 1

time: 586 us -> 586 us (level)
  no operation moved by 1% of the time
where the time goes in v1:
time: 586 us; the launch traced here: 585 us
  local copies, waits for them, and re-layouts  240 us (41%)
  matrix products  168 us (29%)
  waiting for transfers between devices  134 us (23%)
  other arithmetic  23.9 us (4%)
  between operations  13.1 us (2%)
    dot_general x8, matrix products, one_group(): jnp.einsum('kit,jt->kij', stacked, flat_cols, preferred_element_type=jnp....  168 us
    while x56, local copies, waits for them, and re-layouts  159 us
    mul x1, local copies, waits for them, and re-layouts, per_device(): return accumulated_sum * factor  48.4 us
    all_gather x1, waiting for transfers between devices, per_device(): columns = lax.all_gather(col_tiles, 'tm', axis=2, tiled=True)  46.7 us
    all_gather x1, waiting for transfers between devices, collect_rows(): return lax.all_gather(own_window, 'antb', axis=0, tiled=True)  45.1 us
    all_gather x1, waiting for transfers between devices, per_device(): r1 = lax.all_gather(samples, 'anta')  41.4 us
    mul x1, other arithmetic, per_device(): return accumulated_sum * factor  23.9 us
    another operation x8, local copies, waits for them, and re-layouts, one_group(): stacked = jnp.stack(pieces, 0)  22.7 us
  transfers between devices with their start and end apart: 3, of which 3 were waited for; matrix products, arithmetic and copies ran while one was open for 0% of the time, Pallas kernels for 0%

profile of v1, /device:TPU:0, one launch (start us, length us, event | category | flops | bytes accessed | tf_op | source)
XLA Modules:
  0.0 584.9 jit_solution(11511170079034413192)
XLA Ops:
  7.3 41.4 %all-gather.9.cloned.1.call-done = bf16[4,128,1536]{2,1,0:T(8,128)(2,1)} async-done(((bf16[1,128,1536]{2,1,0:T(8,128)(2,1)}), bf16[4,128,1536]{2,1,0:T(8,128)(2,1)}) %all-gather.9.cloned.1.call-update) | async-done | bytes 1572880 | tf_op jit(solution)/shard_map/all_gather | solution.py:41
  48.8 46.7 %all-gather.5.cloned.1.call-done = bf16[1,512,6144]{2,1,0:T(8,128)(2,1)} async-done(((bf16[1,512,1536]{2,1,0:T(8,128)(2,1)}), bf16[1,512,6144]{2,1,0:T(8,128)(2,1)}) %all-gather.5.cloned.1.call-update) | async-done | bytes 6291472 | tf_op jit(solution)/shard_map/all_gather | solution.py:43
  98.2 45.1 %all-gather.7.cloned.1.call-done = bf16[2,128,6144]{2,1,0:T(8,128)(2,1)} async-done(((bf16[1,128,6144]{2,1,0:T(8,128)(2,1)}), bf16[2,128,6144]{2,1,0:T(8,128)(2,1)}) %all-gather.7.cloned.1.call-update) | async-done | bytes 3145744 | tf_op jit(solution)/shard_map/all_gather | solution.py:30
  145.4 360.6 %while.14 = (s32[]{:T(128)}, f32[8,8,256,512]{3,2,1,0:T(8,128)}, s32[8]{0:T(128)S(1)}, s32[]{:T(128)}, bf16[256,6400]{1,0:T(8,128)(2,1)S(1)}, /*index=5*/bf16[51...) while((s32[]{:T(128)}, f32[8,8,256,512]{3,2,1,0:T(8,128)}, ...), condition=%wide.region_1.2_spmd, body=%wide.region_0.1_spmd.sunk | while | flops 12884901888 | bytes 85984392 | solution.py:25
  149.5 2.9 bitcast_dynamic-update-slice_fusion.19
  152.4 2.9 bitcast_dynamic-update-slice_fusion.20
  169.4 21.0 %bitcast_dynamic-update-slice_fusion.26 = f32[8,8,256,512]{3,2,1,0:T(8,128)} fusion(f32[8,8,256,512]{3,2,1,0:T(8,128)} %get-tuple-element.216, s32[]{:T(128)} %get-tuple-element.215, bf16[8,256,6144]{2,1,0:T(8,128)(2,1)} %bitcast_dynamic-update-slice_fusion.25, bf16[512,6144]{1,0:T(8,128)(2,1)} %get-tuple-element.245), kind=kOutput, calls=%fused_computation.2.clone.1 | convolution fusion | flops 12884901888 | bytes 35652096 | tf_op jit(solution)/shard_map/while/body/eval_jaxpr/kit,jt->kij/dot_general | solution.py:23
  194.6 2.9 bitcast_dynamic-update-slice_fusion.19
  197.5 2.9 bitcast_dynamic-update-slice_fusion.20
  214.5 21.1 %bitcast_dynamic-update-slice_fusion.26 = f32[8,8,256,512]{3,2,1,0:T(8,128)} fusion(f32[8,8,256,512]{3,2,1,0:T(8,128)} %get-tuple-element.216, s32[]{:T(128)} %get-tuple-element.215, bf16[8,256,6144]{2,1,0:T(8,128)(2,1)} %bitcast_dynamic-update-slice_fusion.25, bf16[512,6144]{1,0:T(8,128)(2,1)} %get-tuple-element.245), kind=kOutput, calls=%fused_computation.2.clone.1 | convolution fusion | flops 12884901888 | bytes 35652096 | tf_op jit(solution)/shard_map/while/body/eval_jaxpr/kit,jt->kij/dot_general | solution.py:23
  236.8 2.8 bitcast_dynamic-update-slice_fusion.18
  239.7 2.9 bitcast_dynamic-update-slice_fusion.19
  242.6 2.9 bitcast_dynamic-update-slice_fusion.20
  259.6 21.1 %bitcast_dynamic-update-slice_fusion.26 = f32[8,8,256,512]{3,2,1,0:T(8,128)} fusion(f32[8,8,256,512]{3,2,1,0:T(8,128)} %get-tuple-element.216, s32[]{:T(128)} %get-tuple-element.215, bf16[8,256,6144]{2,1,0:T(8,128)(2,1)} %bitcast_dynamic-update-slice_fusion.25, bf16[512,6144]{1,0:T(8,128)(2,1)} %get-tuple-element.245), kind=kOutput, calls=%fused_computation.2.clone.1 | convolution fusion | flops 12884901888 | bytes 35652096 | tf_op jit(solution)/shard_map/while/body/eval_jaxpr/kit,jt->kij/dot_general | solution.py:23
  281.9 2.8 bitcast_dynamic-update-slice_fusion.18
  284.8 2.9 bitcast_dynamic-update-slice_fusion.19
  287.6 2.9 bitcast_dynamic-update-slice_fusion.20
  304.7 21.1 %bitcast_dynamic-update-slice_fusion.26 = f32[8,8,256,512]{3,2,1,0:T(8,128)} fusion(f32[8,8,256,512]{3,2,1,0:T(8,128)} %get-tuple-element.216, s32[]{:T(128)} %get-tuple-element.215, bf16[8,256,6144]{2,1,0:T(8,128)(2,1)} %bitcast_dynamic-update-slice_fusion.25, bf16[512,6144]{1,0:T(8,128)(2,1)} %get-tuple-element.245), kind=kOutput, calls=%fused_computation.2.clone.1 | convolution fusion | flops 12884901888 | bytes 35652096 | tf_op jit(solution)/shard_map/while/body/eval_jaxpr/kit,jt->kij/dot_general | solution.py:23
  329.8 2.9 bitcast_dynamic-update-slice_fusion.19
  332.7 2.9 bitcast_dynamic-update-slice_fusion.20
  349.7 21.1 %bitcast_dynamic-update-slice_fusion.26 = f32[8,8,256,512]{3,2,1,0:T(8,128)} fusion(f32[8,8,256,512]{3,2,1,0:T(8,128)} %get-tuple-element.216, s32[]{:T(128)} %get-tuple-element.215, bf16[8,256,6144]{2,1,0:T(8,128)(2,1)} %bitcast_dynamic-update-slice_fusion.25, bf16[512,6144]{1,0:T(8,128)(2,1)} %get-tuple-element.245), kind=kOutput, calls=%fused_computation.2.clone.1 | convolution fusion | flops 12884901888 | bytes 35652096 | tf_op jit(solution)/shard_map/while/body/eval_jaxpr/kit,jt->kij/dot_general | solution.py:23
  374.9 2.9 bitcast_dynamic-update-slice_fusion.19
  377.8 2.9 bitcast_dynamic-update-slice_fusion.20
  394.8 21.1 %bitcast_dynamic-update-slice_fusion.26 = f32[8,8,256,512]{3,2,1,0:T(8,128)} fusion(f32[8,8,256,512]{3,2,1,0:T(8,128)} %get-tuple-element.216, s32[]{:T(128)} %get-tuple-element.215, bf16[8,256,6144]{2,1,0:T(8,128)(2,1)} %bitcast_dynamic-update-slice_fusion.25, bf16[512,6144]{1,0:T(8,128)(2,1)} %get-tuple-element.245), kind=kOutput, calls=%fused_computation.2.clone.1 | convolution fusion | flops 12884901888 | bytes 35652096 | tf_op jit(solution)/shard_map/while/body/eval_jaxpr/kit,jt->kij/dot_general | solution.py:23
  420.0 2.9 bitcast_dynamic-update-slice_fusion.19
  422.9 2.9 bitcast_dynamic-update-slice_fusion.20
  439.9 21.1 %bitcast_dynamic-update-slice_fusion.26 = f32[8,8,256,512]{3,2,1,0:T(8,128)} fusion(f32[8,8,256,512]{3,2,1,0:T(8,128)} %get-tuple-element.216, s32[]{:T(128)} %get-tuple-element.215, bf16[8,256,6144]{2,1,0:T(8,128)(2,1)} %bitcast_dynamic-update-slice_fusion.25, bf16[512,6144]{1,0:T(8,128)(2,1)} %get-tuple-element.245), kind=kOutput, calls=%fused_computation.2.clone.1 | convolution fusion | flops 12884901888 | bytes 35652096 | tf_op jit(solution)/shard_map/while/body/eval_jaxpr/kit,jt->kij/dot_general | solution.py:23
  465.1 2.9 bitcast_dynamic-update-slice_fusion.19
  467.9 2.9 bitcast_dynamic-update-slice_fusion.20
  485.0 21.1 %bitcast_dynamic-update-slice_fusion.26 = f32[8,8,256,512]{3,2,1,0:T(8,128)} fusion(f32[8,8,256,512]{3,2,1,0:T(8,128)} %get-tuple-element.216, s32[]{:T(128)} %get-tuple-element.215, bf16[8,256,6144]{2,1,0:T(8,128)(2,1)} %bitcast_dynamic-update-slice_fusion.25, bf16[512,6144]{1,0:T(8,128)(2,1)} %get-tuple-element.245), kind=kOutput, calls=%fused_computation.2.clone.1 | convolution fusion | flops 12884901888 | bytes 35652096 | tf_op jit(solution)/shard_map/while/body/eval_jaxpr/kit,jt->kij/dot_general | solution.py:23
  506.0 23.9 %broadcast_multiply_fusion = f32[8,8,256,512]{3,2,1,0:T(8,128)} fusion(f32[8,8,256,512]{3,2,1,0:T(8,128)} %get-tuple-element.140), kind=kLoop, calls=%fused_computation.11 | loop fusion | flops 8388608 | bytes 67108864 | tf_op jit(solution)/shard_map/mul | solution.py:55
  530.0 48.4 %mul.39 = f32[64,2,128,1,512]{4,3,2,1,0:T(1,128)} reshape(f32[8,8,256,512]{3,2,1,0:T(8,128)} %broadcast_multiply_fusion) | data formatting | bytes 67108864 | tf_op jit(solution)/shard_map/mul | solution.py:55
  (64 shorter events, 141.0 us)
Async XLA Ops:
  6.5 42.1 %all-gather.9.cloned.1.call-start = ((), (), s32[]{:S(2)}) async-start(), calls=%async_computation.2 | async-start | bytes 1966080 | tf_op jit(solution)/shard_map/all_gather | solution.py:41
  7.3 88.2 %all-gather.5.cloned.1.call-start = ((), (), s32[]{:S(2)}) async-start(), calls=%async_computation | async-start | bytes 7864320 | tf_op jit(solution)/shard_map/all_gather | solution.py:43
  48.7 94.6 %all-gather.7.cloned.1.call-start = ((), (), s32[]{:S(2)}) async-start(), calls=%async_computation.1 | async-start | bytes 4718592 | tf_op jit(solution)/shard_map/all_gather | solution.py:30
Sparse Core Ops, SparseCore 0:
  8.9 39.7 all-gather.8
  50.2 45.2 all-gather.4
  98.3 44.9 all-gather.6
